TPU v7x, 32 devices: a whole 2x2x4 slice. The times are simulated.
32 devices in a mesh: ctx: 16 (over z, y, core), head: 2 (over x).
Axes of the slice: x: 2, y: 2, z: 4, core: 2. Of those that a mesh axis runs over, the one named last changes fastest.
Arguments:
- patch_hidden: bfloat16 [1024, 4096], P('ctx', 'head'), may hold values from -6 to 6
- queries: bfloat16 [1024, 32, 128], P('ctx', 'head'), may hold values from -6 to 6
- new_keys: bfloat16 [1024, 32, 128], P('ctx', 'head'), may hold values from -6 to 6
- new_values: bfloat16 [1024, 32, 128], P('ctx', 'head'), may hold values from -6 to 6
- cache_keys: bfloat16 [16384, 32, 128], P('ctx', 'head'), may hold values from -6 to 6
- cache_values: bfloat16 [16384, 32, 128], P('ctx', 'head'), may hold values from -6 to 6
- cache_request: int32 [16384], P('ctx'), may hold values from 0 to 7, never falling along the last dimension, each value on 1 to 4096 neighbouring positions
- new_request: int32 [1024], replicated, may hold values from 0 to 7, as said below
- out_weight: bfloat16 [32, 128, 4096], P('head'), may hold values from -0.375 to 0.375
- norm_gain: float32 [4096], replicated, may hold values from 0.1 to 1.9
- dec_kv_weight: bfloat16 [4096, 2, 1024], P(None, None, 'head'), may hold values from -0.09375 to 0.09375
- dec_query_weight: bfloat16 [1024, 1024], P(None, 'head'), may hold values from -0.1875 to 0.1875
- query_gain: float32 [64], replicated, may hold values from 0.1 to 1.9
- key_gain: float32 [64], replicated, may hold values from 0.1 to 1.9
- dec_out_weight: bfloat16 [1024, 1024], P('head'), may hold values from -0.75 to 0.75
- byte_states: bfloat16 [4096, 1024], P('ctx'), may hold values from -6 to 6
- byte_patch: int32 [4096], P('ctx'), may hold values from 0 to 1023, never falling along the last dimension, each value on 1 to 8 neighbouring positions
Outputs:
- patch_out: bfloat16 [1024, 4096], P('ctx', 'head')
- byte_out: bfloat16 [4096, 1024], P('ctx', 'head')
Inputs may be any that keep to these rules, and one draw needn't show every extreme that they name: `new_request`: never falls along the patches; every request of 0 to 7 has an even number, two or more, of new patches. `cache_request`: never falls along the cached patches; every request has one or more cached patches. `byte_patch`: never falls along the bytes; every new patch owns one or more bytes.
All inputs are finite; a program needn't handle non-finite values.
Results may differ from a plain program's by a relative error of at most 0.017.
Values may be sent and summed in bfloat16 or wider, within the bound.
No kernel may reach another device: no remote copies, remote signals or barrier semaphores. Data moves between devices by JAX's collectives and lax.ppermute only.
A program may use at most 128 MiB of HBM per device.

v0:
```python
import jax
import jax.numpy as jnp
from jax import lax
from jax.sharding import PartitionSpec as P

DEC_DH = 64


def row_norm(values, gain_values, epsilon):
    meansq = jnp.mean(values * values, axis=-1, keepdims=True)
    return values * lax.rsqrt(meansq + epsilon) * gain_values


def per_device(
    patch_hidden,
    queries,
    new_keys,
    new_values,
    cache_keys,
    cache_values,
    cache_request,
    new_request,
    out_weight,
    norm_gain,
    dec_kv_weight,
    dec_query_weight,
    query_gain,
    key_gain,
    dec_out_weight,
    byte_states,
    byte_patch,
):
    new_rows, local_heads, head_size = queries.shape
    cache_rows = cache_keys.shape[0]
    total_rows = new_request.shape[0]
    ctx_index = lax.axis_index("ctx")
    head_index = lax.axis_index("head")
    first_new = ctx_index * new_rows
    all_keys = jnp.transpose(jnp.concatenate([cache_keys, new_keys], 0), (1, 0, 2))
    all_values = jnp.transpose(jnp.concatenate([cache_values, new_values], 0), (1, 0, 2))
    own_request = lax.dynamic_slice_in_dim(new_request, first_new, new_rows)
    local_request = jnp.concatenate([cache_request, own_request])
    local_position = jnp.concatenate(
        [jnp.full((cache_rows,), -1, jnp.int32), first_new + jnp.arange(new_rows, dtype=jnp.int32)]
    )
    score_scale = head_size ** (-0.5)
    portion = lax.all_gather(queries, "ctx", axis=0, tiled=True)
    row_count = portion.shape[0]
    piece_index = jnp.arange(row_count, dtype=jnp.int32)
    visible = (local_request[None, :] == new_request[:, None]) & (
        local_position[None, :] <= piece_index[:, None]
    )

    def one_head(inputs):
        query_head, key_head, value_head = inputs
        scores = (
            jnp.einsum("qd,kd->qk", query_head, key_head, preferred_element_type=jnp.float32)
            * score_scale
        )
        highest = jnp.max(jnp.where(visible, scores, -1e30), axis=1)
        weights = jnp.where(visible, jnp.exp(scores - highest[:, None]), 0.0)
        mixed_rows = jnp.dot(
            weights.astype(jnp.bfloat16), value_head, preferred_element_type=jnp.float32
        )
        return (mixed_rows, jnp.sum(weights, axis=1), highest)

    pieces = lax.map(one_head, (jnp.transpose(portion, (1, 0, 2)), all_keys, all_values))
    partial_out, partial_total, partial_max = tuple((part_values for part_values in pieces))
    highest = lax.pmax(partial_max, "ctx")
    factor = jnp.exp(partial_max - highest)
    summed_out, summed_total = (
        lax.psum_scatter(partial_out * factor[..., None], "ctx", scatter_dimension=1, tiled=True),
        lax.psum_scatter(partial_total * factor, "ctx", scatter_dimension=1, tiled=True),
    )
    attended = (summed_out / summed_total[..., None]).astype(jnp.bfloat16)
    flattened = jnp.transpose(attended, (1, 0, 2)).reshape(new_rows, local_heads * head_size)
    head_terms = jnp.dot(
        flattened,
        out_weight.reshape(local_heads * head_size, -1),
        preferred_element_type=jnp.float32,
    )
    model_width = head_terms.shape[1]
    slice_width = patch_hidden.shape[1]
    projected = lax.psum_scatter(head_terms, "head", scatter_dimension=1, tiled=True)
    patch_out = (patch_hidden.astype(jnp.float32) + projected).astype(jnp.bfloat16)
    widened = patch_out.astype(jnp.float32)
    squares = lax.psum(jnp.sum(widened * widened, axis=1), "head")
    gain_part = lax.dynamic_slice_in_dim(norm_gain, head_index * slice_width, slice_width)
    normed_part = (widened * lax.rsqrt(squares / model_width + 1e-05)[:, None] * gain_part).astype(
        jnp.bfloat16
    )
    normed = lax.all_gather(normed_part, "head", axis=1, tiled=True)
    dec_width = dec_kv_weight.shape[2]
    dec_heads = dec_width // DEC_DH
    patch_proj = jnp.dot(
        normed,
        dec_kv_weight.reshape(dec_kv_weight.shape[0], 2 * dec_width),
        preferred_element_type=jnp.float32,
    )
    patch_keys = row_norm(
        patch_proj[:, :dec_width].reshape(new_rows, dec_heads, DEC_DH), key_gain, 1e-06
    ).astype(jnp.bfloat16)
    patch_values = (
        patch_proj[:, dec_width:].astype(jnp.bfloat16).reshape(new_rows, dec_heads, DEC_DH)
    )
    byte_rows = byte_states.shape[0]
    query_proj = jnp.dot(byte_states, dec_query_weight, preferred_element_type=jnp.float32).reshape(
        byte_rows, dec_heads, DEC_DH
    )
    byte_query = row_norm(query_proj, query_gain, 1e-06).astype(jnp.bfloat16)
    table_index = jnp.arange(total_rows, dtype=jnp.int32)
    owner_table = table_index[None, :] == byte_patch[:, None]
    byte_request = jnp.sum(jnp.where(owner_table, new_request[None, :], 0), axis=1)
    dec_scale = DEC_DH ** (-0.5)
    piece_keys = lax.all_gather(patch_keys, "ctx", axis=0, tiled=True)
    piece_values = lax.all_gather(patch_values, "ctx", axis=0, tiled=True)
    row_count = piece_keys.shape[0]
    patch_index = jnp.arange(row_count, dtype=jnp.int32)
    fold_visible = (new_request[None, :] == byte_request[:, None]) & (
        patch_index[None, :] <= byte_patch[:, None]
    )
    scores = (
        jnp.einsum("bhd,jhd->hbj", byte_query, piece_keys, preferred_element_type=jnp.float32)
        * dec_scale
    )
    weights = jnp.where(fold_visible[None], jnp.exp(scores), 0.0)
    mixed_rows = jnp.einsum(
        "hbj,jhd->bhd",
        weights.astype(jnp.bfloat16),
        piece_values,
        preferred_element_type=jnp.float32,
    )
    denominator = jnp.transpose(jnp.sum(weights, axis=2))
    byte_mixed = (
        (mixed_rows / denominator[..., None]).astype(jnp.bfloat16).reshape(byte_rows, dec_width)
    )
    byte_terms = jnp.dot(byte_mixed, dec_out_weight, preferred_element_type=jnp.float32)
    byte_sum = lax.psum_scatter(byte_terms, "head", scatter_dimension=1, tiled=True)
    out_width = byte_sum.shape[1]
    own_states = lax.dynamic_slice_in_dim(byte_states, head_index * out_width, out_width, 1)
    byte_out = (own_states.astype(jnp.float32) + byte_sum).astype(jnp.bfloat16)
    return (patch_out, byte_out)


def solution(mesh):
    placed = (
        P("ctx", "head"),
        P("ctx", "head", None),
        P("ctx", "head", None),
        P("ctx", "head", None),
        P("ctx", "head", None),
        P("ctx", "head", None),
        P("ctx"),
        P(),
        P("head", None, None),
        P(),
        P(None, None, "head"),
        P(None, "head"),
        P(),
        P(),
        P("head", None),
        P("ctx", None),
        P("ctx"),
    )
    return jax.shard_map(
        per_device,
        mesh=mesh,
        in_specs=placed,
        out_specs=(P("ctx", "head"), P("ctx", "head")),
        check_vma=False,
    )
```

profile of v0, /device:TPU:0, one launch (start us, length us, event | category | flops | bytes accessed | tf_op | source)
XLA Modules:
  0.0 629.6 jit_solution(7363839396870362774)
XLA Ops:
  9.2 5.4 copy.45
  14.6 3.1 copy.47
  18.0 6.0 maximum_bitcast_fusion
  24.0 39.9 %all-gather.4.cloned.1.call-done = bf16[1024,16,128]{2,0,1:T(8,128)(2,1)} async-done(((bf16[64,16,128]{2,0,1:T(8,128)(2,1)}), bf16[1024,16,128]{2,0,1:T(8,128)(2,1)}) %all-gather.4.cloned.1.call-update) | async-done | bytes 4194320 | tf_op jit(solution)/shard_map/all_gather | solution.py:47
  63.9 143.5 %while.15 = (s32[]{:T(128)}, f32[16,1024,128]{2,1,0:T(8,128)}, f32[16,1024]{1,0:T(8,128)S(1)}, f32[16,1024]{1,0:T(8,128)}, bf16[16,1024,128]{2,1,0:T(8,128)(2,1)...) while((s32[]{:T(128)}, f32[16,1024,128]{2,1,0:T(8,128)}, ...), condition=%wide.region_3.4_spmd.clone, body=%wide.region_0.3_spmd.clone.sunk | while | flops 590477312 | bytes 14786173 | solution.py:67
  63.9 2.5 select_reduce_fusion.3
  66.4 3.4 fusion.74
  72.9 2.5 select_reduce_fusion.3
  75.4 3.4 fusion.74
  81.8 2.5 select_reduce_fusion.3
  84.3 3.4 fusion.74
  93.3 3.4 fusion.74
  99.7 2.5 select_reduce_fusion.3
  102.2 3.4 fusion.74
  108.7 2.5 select_reduce_fusion.3
  111.2 3.4 fusion.74
  117.7 2.5 select_reduce_fusion.3
  120.2 3.4 fusion.74
  129.1 3.4 fusion.74
  135.6 2.5 select_reduce_fusion.3
  138.1 3.4 fusion.74
  144.6 2.5 select_reduce_fusion.3
  147.1 3.4 fusion.74
  156.0 3.4 fusion.74
  162.5 2.5 select_reduce_fusion.3
  165.0 3.4 fusion.74
  171.5 2.5 select_reduce_fusion.3
  174.0 3.4 fusion.74
  180.4 2.5 select_reduce_fusion.3
  182.9 3.4 fusion.74
  191.9 3.4 fusion.74
  198.4 2.5 select_reduce_fusion.3
  200.9 3.4 fusion.74
  207.4 84.9 %all-reduce.3.cloned.1.call-done = f32[16,1024]{1,0:T(8,128)} async-done(((f32[16,1024]{1,0:T(8,128)}), f32[16,1024]{1,0:T(8,128)}) %all-reduce.3.cloned.1.call-update) | async-done | bytes 65552 | tf_op jit(solution)/shard_map/pmax | solution.py:69
  294.3 7.9 %broadcast_multiply_fusion = f32[16,1024,128]{2,1,0:T(8,128)} fusion(f32[16,1024,128]{2,1,0:T(8,128)} %get-tuple-element.46, f32[16,1024]{1,0:T(8,128)S(1)} %get-tuple-element.97), kind=kLoop, calls=%fused_computation.29 | loop fusion | flops 2097152 | bytes 16842752 | tf_op jit(solution)/shard_map/mul | solution.py:72
  302.3 51.3 %reduce-scatter.13.cloned.1.call-done = f32[64,16]{1,0:T(8,128)} async-done(((f32[1024,16]{1,0:T(8,128)}), f32[64,16]{1,0:T(8,128)}) %reduce-scatter.13.cloned.1.call-update) | async-done | bytes 4112
  354.5 105.9 %reduce-scatter.7.cloned.1.call-done = f32[16,64,128]{2,1,0:T(8,128)} async-done(((f32[16,1024,128]{2,1,0:T(8,128)}), f32[16,64,128]{2,1,0:T(8,128)}) %reduce-scatter.7.cloned.1.call-update) | async-done | bytes 524304 | tf_op jit(solution)/shard_map/reduce_scatter | solution.py:72
  460.3 10.1 %convolution_bitcast_fusion = f32[64,4096]{1,0:T(8,128)} fusion(bf16[16,128,4096]{2,1,0:T(8,128)(2,1)} %param.27, f32[16,64,128]{2,1,0:T(8,128)} %reduce-scatter.7.cloned.1.call-done, f32[16,64]{1,0:T(8,128)S(1)} %copy.55), kind=kOutput, calls=%fused_computation.23 | convolution fusion | flops 1074003968 | bytes 18354176 | tf_op jit(solution)/shard_map/dot_general | solution.py:77
  470.7 9.4 %copy.56 = bf16[512,8,2,512]{3,1,2,0:T(8,128)(2,1)} copy(bf16[512,8,2,512]{3,2,1,0:T(2,128)(2,1)} %bitcast.64) | data formatting | bytes 16777216
  480.1 10.5 %reduce-scatter.9.cloned.1.call-done = f32[64,2048]{1,0:T(8,128)} async-done(((f32[64,4096]{1,0:T(8,128)}), f32[64,2048]{1,0:T(8,128)}) %reduce-scatter.9.cloned.1.call-update) | async-done | bytes 524304 | tf_op jit(solution)/shard_map/reduce_scatter | solution.py:84
  491.9 4.9 psum.7
  496.9 7.4 %all_gather.13 = bf16[64,4096]{1,0:T(8,128)(2,1)S(1)} all-gather(bf16[64,2048]{1,0:T(8,128)(2,1)S(1)} %fusion.48), channel_id=1, replica_groups=mesh['ctx'=16,'head'=2] {'head'}, dimensions={1}, use_global_device_ids=true | all-gather | bytes 786432 | tf_op jit(solution)/shard_map/all_gather | solution.py:92
  504.4 5.1 fusion.58
  512.8 39.5 %all-gather.8.cloned.1.call-done = bf16[1024,8,64]{2,0,1:T(8,128)(2,1)} async-done(((bf16[64,8,64]{2,0,1:T(8,128)(2,1)}), bf16[1024,8,64]{2,0,1:T(8,128)(2,1)}) %all-gather.8.cloned.1.call-update) | async-done | bytes 1048592 | tf_op jit(solution)/shard_map/all_gather | solution.py:115
  552.3 7.1 %fusion.22 = (f32[8,256]{1,0:T(8,128)S(1)}, f32[8,256,1024]{2,1,0:T(8,128)}) fusion(pred[256,1024]{1,0:T(8,128)(4,1)S(1)} %fusion.35, bf16[1024,8,64]{2,0,1:T(8,128)(2,1)} %all-gather.8.cloned.1.call-done, f32[256,8,64]{0,2,1:T(8,128)S(1)} %bitcast.66, f32[64]{0:T(128)S(1)} %copy-done.13, f32[256,8]{0,1:T(8,128)S(1)} %add_rsqrt_fusion), kind=kOutput, calls=%fused_computation.21 | convolution fusion | flops 275118080 | bytes 10240256 | tf_op jit(solution)/shard_map/bhd,jhd->hbj/dot_general | solution.py:123
  559.4 35.3 %all-gather.6.cloned.1.call-done = bf16[1024,8,64]{2,1,0:T(8,128)(2,1)} async-done(((bf16[64,8,64]{2,1,0:T(8,128)(2,1)}), bf16[1024,8,64]{2,1,0:T(8,128)(2,1)}) %all-gather.6.cloned.1.call-update) | async-done | bytes 1048592 | tf_op jit(solution)/shard_map/all_gather | solution.py:116
  594.7 5.5 fusion.41
  601.7 19.2 %reduce-scatter.11.cloned.1.call-done = f32[256,512]{1,0:T(8,128)} async-done(((f32[256,1024]{1,0:T(8,128)}), f32[256,512]{1,0:T(8,128)}) %reduce-scatter.11.cloned.1.call-update) | async-done | bytes 524304 | tf_op jit(solution)/shard_map/reduce_scatter | solution.py:138
  (127 shorter events, 72.0 us)
Async XLA Ops:
  7.2 593.1 %copy-start = (bf16[512,1024]{1,0:T(8,128)(2,1)S(1)}, bf16[512,1024]{1,0:T(8,128)(2,1)}, u32[]{:S(2)}) copy-start(bf16[512,1024]{1,0:T(8,128)(2,1)} %param.33) | copy-start | bytes 3145732
  7.2 56.7 %all-gather.4.cloned.1.call-start = ((), (), s32[]{:S(2)}) async-start(), calls=%async_computation.4 | async-start | bytes 4456448 | tf_op jit(solution)/shard_map/all_gather | solution.py:47
  9.1 283.3 %all-reduce.3.cloned.1.call-start = ((), (), s32[]{:S(2)}) async-start(), calls=%async_computation.5 | async-start | bytes 131072 | tf_op jit(solution)/shard_map/pmax | solution.py:69
  9.1 5.5 copy-start.1
  14.6 3.1 copy-start.5
  14.6 3.2 copy-start.6
  14.6 3.3 copy-start.8
  14.6 3.4 copy-start.10
  207.4 146.2 %reduce-scatter.13.cloned.1.call-start = ((), (), s32[]{:S(2)}) async-start(), calls=%async_computation.11 | async-start | bytes 557056
  294.3 166.0 %reduce-scatter.7.cloned.1.call-start = ((), (), s32[]{:S(2)}) async-start(), calls=%async_computation.6 | async-start | bytes 8912896 | tf_op jit(solution)/shard_map/reduce_scatter | solution.py:72
  302.3 188.3 %reduce-scatter.9.cloned.1.call-start = ((), (), s32[]{:S(2)}) async-start(), calls=%async_computation.7 | async-start | bytes 1572864 | tf_op jit(solution)/shard_map/reduce_scatter | solution.py:84
  470.4 81.8 %all-gather.8.cloned.1.call-start = ((), (), s32[]{:S(2)}) async-start(), calls=%async_computation.9 | async-start | bytes 2228224 | tf_op jit(solution)/shard_map/all_gather | solution.py:115
  470.7 9.4 %copy-start.11 = (f32[4096]{0:T(1024)S(1)}, f32[4096]{0:T(1024)}, u32[]{:S(2)}) copy-start(f32[4096]{0:T(1024)} %param.28) | copy-start | bytes 49156
  470.7 19.9 %copy-start.7 = (bf16[64,2048]{1,0:T(8,128)(2,1)S(1)}, bf16[64,2048]{1,0:T(8,128)(2,1)}, u32[]{:S(2)}) copy-start(bf16[64,2048]{1,0:T(8,128)(2,1)} %param.19) | copy-start | bytes 786436
  491.8 17.6 %copy-start.4 = (bf16[64,2048]{1,0:T(8,128)(2,1)}, bf16[64,2048]{1,0:T(8,128)(2,1)S(1)}, u32[]{:S(2)}) copy-start(bf16[64,2048]{1,0:T(8,128)(2,1)S(1)} %get-tuple-element.95) | copy-start | bytes 786436
  504.3 5.5 copy-start.12
  504.3 7.2 %copy-start.9 = (s32[256]{0:T(256)S(1)}, s32[256]{0:T(256)}, u32[]{:S(2)}) copy-start(s32[256]{0:T(256)} %param.35) | copy-start | bytes 3076
  504.3 7.5 %copy-start.2 = (bf16[256,1024]{1,0:T(8,128)(2,1)S(1)}, bf16[256,1024]{1,0:T(8,128)(2,1)}, u32[]{:S(2)}) copy-start(bf16[256,1024]{1,0:T(8,128)(2,1)} %param.34) | copy-start | bytes 1572868
  504.3 7.5 %copy-start.3 = (bf16[1024,512]{1,0:T(8,128)(2,1)S(1)}, bf16[1024,512]{1,0:T(8,128)(2,1)}, u32[]{:S(2)}) copy-start(bf16[1024,512]{1,0:T(8,128)(2,1)} %param.30) | copy-start | bytes 3145732
  504.3 47.9 %copy-start.13 = (f32[64]{0:T(128)S(1)}, f32[64]{0:T(128)}, u32[]{:S(2)}) copy-start(f32[64]{0:T(128)} %param.31) | copy-start | bytes 772
  510.6 84.0 %all-gather.6.cloned.1.call-start = ((), (), s32[]{:S(2)}) async-start(), calls=%async_computation.8 | async-start | bytes 2228224 | tf_op jit(solution)/shard_map/all_gather | solution.py:116
  511.5 109.4 %reduce-scatter.11.cloned.1.call-start = ((), (), s32[]{:S(2)}) async-start(), calls=%async_computation.10 | async-start | bytes 1572864 | tf_op jit(solution)/shard_map/reduce_scatter | solution.py:138
Sparse Core Ops, SparseCore 0:
  10.7 53.1 all-gather.3
  207.5 84.7 all-reduce.2
  295.9 57.6 reduce-scatter.12
  357.6 102.7 reduce-scatter.6
  470.6 20.0 reduce-scatter.8
  510.8 41.4 all-gather.7
  554.4 40.1 all-gather.5
  601.8 19.0 reduce-scatter.10
where the time goes:
time: 632 us; the launch traced here: 630 us
  waiting for transfers between devices  387 us (61%)
  matrix products  124 us (20%)
  local copies, waits for them, and re-layouts  46.9 us (7%)
  other arithmetic  44.4 us (7%)
  between operations  14.4 us (2%)
  blocking collectives  12.3 us (2%)
    reduce_scatter x1, waiting for transfers between devices, per_device(): lax.psum_scatter(partial_out * factor[..., None], 'ctx', scatter_dimensio...  106 us
    pmax x1, waiting for transfers between devices, per_device(): highest = lax.pmax(partial_max, 'ctx')  84.9 us
    dot_general x16, matrix products, one_head(): jnp.dot(weights.astype(jnp.bfloat16), value_head, preferred_element_type=...  54.4 us
    unnamed x9, waiting for transfers between devices  51.4 us
    all_gather x1, waiting for transfers between devices, per_device(): portion = lax.all_gather(queries, 'ctx', axis=0, tiled=True)  39.9 us
    dot_general x16, matrix products, one_head(): jnp.einsum('qd,kd->qk', query_head, key_head, preferred_element_type=jnp....  39.8 us
    all_gather x1, waiting for transfers between devices, per_device(): piece_keys = lax.all_gather(patch_keys, 'ctx', axis=0, tiled=True)  39.5 us
    all_gather x1, waiting for transfers between devices, per_device(): piece_values = lax.all_gather(patch_values, 'ctx', axis=0, tiled=True)  35.3 us
  transfers between devices with their start and end apart: 8, of which 8 were waited for; matrix products, arithmetic and copies ran while one was open for 7% of the time, Pallas kernels for 0%

commit v1 on v0

--- a/solution.py
+++ b/solution.py
@@ -112,7 +112,13 @@
     owner_table = table_index[None, :] == byte_patch[:, None]
     byte_request = jnp.sum(jnp.where(owner_table, new_request[None, :], 0), axis=1)
     dec_scale = DEC_DH ** (-0.5)
-    piece_keys = lax.all_gather(patch_keys, "ctx", axis=0, tiled=True)
+    peers = lax.axis_size("ctx")
+    current, parts = (patch_keys, [patch_keys])
+    for _ in range(peers - 1):
+        current = lax.ppermute(current, "ctx", [(i, (i + 1) % peers) for i in range(peers)])
+        parts.insert(0, current)
+    flat = jnp.concatenate(parts, axis=0)
+    piece_keys = jnp.roll(flat, (lax.axis_index("ctx") + 1) * patch_keys.shape[0], axis=0)
     piece_values = lax.all_gather(patch_values, "ctx", axis=0, tiled=True)
     row_count = piece_keys.shape[0]
     patch_index = jnp.arange(row_count, dtype=jnp.int32)

time: 632 us -> 673 us (1.065)
  waiting for transfers between devices: 387 us -> 414 us
  local copies, waits for them, and re-layouts: 46.9 us -> 60.4 us
    ppermute x0 -> x15, waiting for transfers between devices: none -> 103 us  [per_device(): lax.ppermute(current, 'ctx', [(i, (i + 1) % peers) for i in range(peers)])]
    all_gather x1 -> x0, waiting for transfers between devices: 39.5 us -> none  [per_device(): piece_keys = lax.all_gather(patch_keys, 'ctx', axis=0, tiled=True)]
    all_gather x1, waiting for transfers between devices: 35.3 us -> 0.01 us  [per_device(): piece_values = lax.all_gather(patch_values, 'ctx', axis=0, tiled=True)]
    unnamed x36 -> x66, local copies, waits for them, and re-layouts: 21.7 us -> 28.3 us
    unnamed x9 -> x8, waiting for transfers between devices: 51.4 us -> 51.4 us
  transfers between devices with their start and end apart: 8 -> 22, of which waited for: 8 -> 21; matrix products, arithmetic and copies ran while one was open for 7% -> 7% of each run, Pallas kernels for 0% -> 0%
where the time goes in v1:
time: 673 us; the launch traced here: 671 us
  waiting for transfers between devices  414 us (62%)
  matrix products  124 us (18%)
  local copies, waits for them, and re-layouts  60.4 us (9%)
  other arithmetic  44.5 us (7%)
  between operations  14.5 us (2%)
  blocking collectives  12.3 us (2%)
    reduce_scatter x1, waiting for transfers between devices, per_device(): lax.psum_scatter(partial_out * factor[..., None], 'ctx', scatter_dimensio...  106 us
    ppermute x15, waiting for transfers between devices, per_device(): lax.ppermute(current, 'ctx', [(i, (i + 1) % peers) for i in range(peers)])  103 us
    pmax x1, waiting for transfers between devices, per_device(): highest = lax.pmax(partial_max, 'ctx')  84.9 us
    dot_general x16, matrix products, one_head(): jnp.dot(weights.astype(jnp.bfloat16), value_head, preferred_element_type=...  54.4 us
    unnamed x8, waiting for transfers between devices  51.4 us
    dot_general x16, matrix products, one_head(): jnp.einsum('qd,kd->qk', query_head, key_head, preferred_element_type=jnp....  39.8 us
    all_gather x1, waiting for transfers between devices, per_device(): portion = lax.all_gather(queries, 'ctx', axis=0, tiled=True)  39.8 us
    unnamed x66, local copies, waits for them, and re-layouts  28.3 us
  transfers between devices with their start and end apart: 22, of which 21 were waited for; matrix products, arithmetic and copies ran while one was open for 7% of the time, Pallas kernels for 0%

profile of v1, /device:TPU:0, one launch (start us, length us, event | category | flops | bytes accessed | tf_op | source)
XLA Modules:
  0.0 670.6 jit_solution(14817436686621902664)
XLA Ops:
  9.2 5.4 copy.45
  18.0 6.1 maximum_bitcast_fusion
  24.1 39.8 %all-gather.3.cloned.1.call-done = bf16[1024,16,128]{2,0,1:T(8,128)(2,1)} async-done(((bf16[64,16,128]{2,0,1:T(8,128)(2,1)}), bf16[1024,16,128]{2,0,1:T(8,128)(2,1)}) %all-gather.3.cloned.1.call-update) | async-done | bytes 4194320 | tf_op jit(solution)/shard_map/all_gather | solution.py:47
  63.9 143.5 %while.15 = (s32[]{:T(128)}, f32[16,1024,128]{2,1,0:T(8,128)}, f32[16,1024]{1,0:T(8,128)S(1)}, f32[16,1024]{1,0:T(8,128)}, bf16[16,1024,128]{2,1,0:T(8,128)(2,1)...) while((s32[]{:T(128)}, f32[16,1024,128]{2,1,0:T(8,128)}, ...), condition=%wide.region_3.4_spmd.clone, body=%wide.region_0.3_spmd.clone.sunk | while | flops 590477312 | bytes 14786173 | solution.py:67
  66.4 3.4 fusion.67
  75.3 3.4 fusion.67
  84.3 3.4 fusion.67
  93.3 3.4 fusion.67
  102.2 3.4 fusion.67
  111.2 3.4 fusion.67
  120.2 3.4 fusion.67
  129.1 3.4 fusion.67
  138.1 3.4 fusion.67
  147.1 3.4 fusion.67
  156.0 3.4 fusion.67
  165.0 3.4 fusion.67
  174.0 3.4 fusion.67
  191.9 3.4 fusion.67
  200.8 3.4 fusion.67
  207.4 84.9 %all-reduce.3.cloned.1.call-done = f32[16,1024]{1,0:T(8,128)} async-done(((f32[16,1024]{1,0:T(8,128)}), f32[16,1024]{1,0:T(8,128)}) %all-reduce.3.cloned.1.call-update) | async-done | bytes 65552 | tf_op jit(solution)/shard_map/pmax | solution.py:69
  294.3 7.9 %broadcast_multiply_fusion = f32[16,1024,128]{2,1,0:T(8,128)} fusion(f32[16,1024,128]{2,1,0:T(8,128)} %get-tuple-element.46, f32[16,1024]{1,0:T(8,128)S(1)} %get-tuple-element.97), kind=kLoop, calls=%fused_computation.29 | loop fusion | flops 2097152 | bytes 16842752 | tf_op jit(solution)/shard_map/mul | solution.py:72
  302.3 51.3 %reduce-scatter.13.cloned.1.call-done = f32[64,16]{1,0:T(8,128)} async-done(((f32[1024,16]{1,0:T(8,128)}), f32[64,16]{1,0:T(8,128)}) %reduce-scatter.13.cloned.1.call-update) | async-done | bytes 4112
  354.4 105.9 %reduce-scatter.7.cloned.1.call-done = f32[16,64,128]{2,1,0:T(8,128)} async-done(((f32[16,1024,128]{2,1,0:T(8,128)}), f32[16,64,128]{2,1,0:T(8,128)}) %reduce-scatter.7.cloned.1.call-update) | async-done | bytes 524304 | tf_op jit(solution)/shard_map/reduce_scatter | solution.py:72
  460.3 10.1 %convolution_bitcast_fusion = f32[64,4096]{1,0:T(8,128)} fusion(bf16[16,128,4096]{2,1,0:T(8,128)(2,1)} %param.27, f32[16,64,128]{2,1,0:T(8,128)} %reduce-scatter.7.cloned.1.call-done, f32[16,64]{1,0:T(8,128)S(1)} %copy.55), kind=kOutput, calls=%fused_computation.23 | convolution fusion | flops 1074003968 | bytes 18354176 | tf_op jit(solution)/shard_map/dot_general | solution.py:77
  470.7 9.4 %copy.56 = bf16[512,8,2,512]{3,1,2,0:T(8,128)(2,1)} copy(bf16[512,8,2,512]{3,2,1,0:T(2,128)(2,1)} %bitcast.61) | data formatting | bytes 16777216
  480.1 10.5 %reduce-scatter.9.cloned.1.call-done = f32[64,2048]{1,0:T(8,128)} async-done(((f32[64,4096]{1,0:T(8,128)}), f32[64,2048]{1,0:T(8,128)}) %reduce-scatter.9.cloned.1.call-update) | async-done | bytes 524304 | tf_op jit(solution)/shard_map/reduce_scatter | solution.py:84
  491.8 4.9 psum.7
  496.9 7.4 %all_gather.10 = bf16[64,4096]{1,0:T(8,128)(2,1)S(1)} all-gather(bf16[64,2048]{1,0:T(8,128)(2,1)S(1)} %fusion.40), channel_id=1, replica_groups=mesh['ctx'=16,'head'=2] {'head'}, dimensions={1}, use_global_device_ids=true | all-gather | bytes 786432 | tf_op jit(solution)/shard_map/all_gather | solution.py:92
  504.3 5.1 fusion.52
  510.8 7.1 %collective-permute-done = bf16[64,8,64]{0,2,1:T(8,128)(2,1)S(1)} collective-permute-done((bf16[64,8,64]{0,2,1:T(8,128)(2,1)S(1)}, bf16[64,8,64]{0,2,1:T(8,128)(2,1)S(1)}, u32[]{:S(2)}, u32[]{:S(2)}) %collective-permute-start) | collective-permute-done | bytes 65568 | tf_op jit(solution)/shard_map/ppermute | solution.py:118
  519.6 5.3 collective-permute-done.1
  524.9 7.2 %collective-permute-done.2 = bf16[64,8,64]{0,2,1:T(8,128)(2,1)S(1)} collective-permute-done((bf16[64,8,64]{0,2,1:T(8,128)(2,1)S(1)}, bf16[64,8,64]{0,2,1:T(8,128)(2,1)S(1)}, u32[]{:S(2)}, u32[]{:S(2)}) %collective-permute-start.2) | collective-permute-done | bytes 65568 | tf_op jit(solution)/shard_map/ppermute | solution.py:118
  532.1 7.8 %collective-permute-done.3 = bf16[64,8,64]{0,2,1:T(8,128)(2,1)S(1)} collective-permute-done((bf16[64,8,64]{0,2,1:T(8,128)(2,1)S(1)}, bf16[64,8,64]{0,2,1:T(8,128)(2,1)S(1)}, u32[]{:S(2)}, u32[]{:S(2)}) %collective-permute-start.3) | collective-permute-done | bytes 65568 | tf_op jit(solution)/shard_map/ppermute | solution.py:118
  539.9 7.1 %collective-permute-done.4 = bf16[64,8,64]{0,2,1:T(8,128)(2,1)S(1)} collective-permute-done((bf16[64,8,64]{0,2,1:T(8,128)(2,1)S(1)}, bf16[64,8,64]{0,2,1:T(8,128)(2,1)S(1)}, u32[]{:S(2)}, u32[]{:S(2)}) %collective-permute-start.4) | collective-permute-done | bytes 65568 | tf_op jit(solution)/shard_map/ppermute | solution.py:118
  547.7 8.3 %collective-permute-done.5 = bf16[64,8,64]{0,2,1:T(8,128)(2,1)S(1)} collective-permute-done((bf16[64,8,64]{0,2,1:T(8,128)(2,1)S(1)}, bf16[64,8,64]{0,2,1:T(8,128)(2,1)S(1)}, u32[]{:S(2)}, u32[]{:S(2)}) %collective-permute-start.5) | collective-permute-done | bytes 65568 | tf_op jit(solution)/shard_map/ppermute | solution.py:118
  556.6 7.1 %collective-permute-done.6 = bf16[64,8,64]{0,2,1:T(8,128)(2,1)S(1)} collective-permute-done((bf16[64,8,64]{0,2,1:T(8,128)(2,1)S(1)}, bf16[64,8,64]{0,2,1:T(8,128)(2,1)S(1)}, u32[]{:S(2)}, u32[]{:S(2)}) %collective-permute-start.6) | collective-permute-done | bytes 65568 | tf_op jit(solution)/shard_map/ppermute | solution.py:118
  564.4 7.1 %collective-permute-done.7 = bf16[64,8,64]{0,2,1:T(8,128)(2,1)S(1)} collective-permute-done((bf16[64,8,64]{0,2,1:T(8,128)(2,1)S(1)}, bf16[64,8,64]{0,2,1:T(8,128)(2,1)S(1)}, u32[]{:S(2)}, u32[]{:S(2)}) %collective-permute-start.7) | collective-permute-done | bytes 65568 | tf_op jit(solution)/shard_map/ppermute | solution.py:118
  572.1 7.1 %collective-permute-done.8 = bf16[64,8,64]{0,2,1:T(8,128)(2,1)S(1)} collective-permute-done((bf16[64,8,64]{0,2,1:T(8,128)(2,1)S(1)}, bf16[64,8,64]{0,2,1:T(8,128)(2,1)S(1)}, u32[]{:S(2)}, u32[]{:S(2)}) %collective-permute-start.8) | collective-permute-done | bytes 65568 | tf_op jit(solution)/shard_map/ppermute | solution.py:118
  579.9 7.1 %collective-permute-done.9 = bf16[64,8,64]{0,2,1:T(8,128)(2,1)S(1)} collective-permute-done((bf16[64,8,64]{0,2,1:T(8,128)(2,1)S(1)}, bf16[64,8,64]{0,2,1:T(8,128)(2,1)S(1)}, u32[]{:S(2)}, u32[]{:S(2)}) %collective-permute-start.9) | collective-permute-done | bytes 65568 | tf_op jit(solution)/shard_map/ppermute | solution.py:118
  587.6 7.1 %collective-permute-done.10 = bf16[64,8,64]{0,2,1:T(8,128)(2,1)S(1)} collective-permute-done((bf16[64,8,64]{0,2,1:T(8,128)(2,1)S(1)}, bf16[64,8,64]{0,2,1:T(8,128)(2,1)S(1)}, u32[]{:S(2)}, u32[]{:S(2)}) %collective-permute-start.10) | collective-permute-done | bytes 65568 | tf_op jit(solution)/shard_map/ppermute | solution.py:118
  596.0 5.7 collective-permute-done.11
  602.7 6.8 %collective-permute-done.12 = bf16[64,8,64]{0,2,1:T(8,128)(2,1)S(1)} collective-permute-done((bf16[64,8,64]{0,2,1:T(8,128)(2,1)S(1)}, bf16[64,8,64]{0,2,1:T(8,128)(2,1)S(1)}, u32[]{:S(2)}, u32[]{:S(2)}) %collective-permute-start.12) | collective-permute-done | bytes 65568 | tf_op jit(solution)/shard_map/ppermute | solution.py:118
  611.3 6.0 collective-permute-done.13
  617.9 6.6 collective-permute-done.14
  624.5 5.9 concatenate.22
  630.4 6.7 fusion.22
  637.1 5.6 divide_convert_fusion
  644.2 17.8 %reduce-scatter.11.cloned.1.call-done = f32[256,512]{1,0:T(8,128)} async-done(((f32[256,1024]{1,0:T(8,128)}), f32[256,512]{1,0:T(8,128)}) %reduce-scatter.11.cloned.1.call-update) | async-done | bytes 524304 | tf_op jit(solution)/shard_map/reduce_scatter | solution.py:144
  (186 shorter events, 116.8 us)
Async XLA Ops:
  7.2 635.5 %copy-start = (bf16[512,1024]{1,0:T(8,128)(2,1)S(1)}, bf16[512,1024]{1,0:T(8,128)(2,1)}, u32[]{:S(2)}) copy-start(bf16[512,1024]{1,0:T(8,128)(2,1)} %param.33) | copy-start | bytes 3145732
  7.2 56.7 %all-gather.3.cloned.1.call-start = ((), (), s32[]{:S(2)}) async-start(), calls=%async_computation.4 | async-start | bytes 4456448 | tf_op jit(solution)/shard_map/all_gather | solution.py:47
  9.1 283.3 %all-reduce.3.cloned.1.call-start = ((), (), s32[]{:S(2)}) async-start(), calls=%async_computation.5 | async-start | bytes 131072 | tf_op jit(solution)/shard_map/pmax | solution.py:69
  9.1 5.4 copy-start.1
  14.6 3.2 copy-start.19
  14.6 3.2 copy-start.20
  14.6 3.3 copy-start.23
  14.6 3.4 copy-start.25
  207.4 146.2 %reduce-scatter.13.cloned.1.call-start = ((), (), s32[]{:S(2)}) async-start(), calls=%async_computation.10 | async-start | bytes 557056
  294.3 166.1 %reduce-scatter.7.cloned.1.call-start = ((), (), s32[]{:S(2)}) async-start(), calls=%async_computation.6 | async-start | bytes 8912896 | tf_op jit(solution)/shard_map/reduce_scatter | solution.py:72
  302.3 188.3 %reduce-scatter.9.cloned.1.call-start = ((), (), s32[]{:S(2)}) async-start(), calls=%async_computation.7 | async-start | bytes 1572864 | tf_op jit(solution)/shard_map/reduce_scatter | solution.py:84
  470.4 166.7 %all-gather.5.cloned.1.call-start = ((), (), s32[]{:S(2)}) async-start(), calls=%async_computation.8 | async-start | bytes 2228224 | tf_op jit(solution)/shard_map/all_gather | solution.py:122
  470.7 9.4 %copy-start.26 = (f32[4096]{0:T(1024)S(1)}, f32[4096]{0:T(1024)}, u32[]{:S(2)}) copy-start(f32[4096]{0:T(1024)} %param.28) | copy-start | bytes 49156
  470.7 19.9 %copy-start.22 = (bf16[64,2048]{1,0:T(8,128)(2,1)S(1)}, bf16[64,2048]{1,0:T(8,128)(2,1)}, u32[]{:S(2)}) copy-start(bf16[64,2048]{1,0:T(8,128)(2,1)} %param.19) | copy-start | bytes 786436
  491.8 17.6 %copy-start.5 = (bf16[64,2048]{1,0:T(8,128)(2,1)}, bf16[64,2048]{1,0:T(8,128)(2,1)S(1)}, u32[]{:S(2)}) copy-start(bf16[64,2048]{1,0:T(8,128)(2,1)S(1)} %get-tuple-element.95) | copy-start | bytes 786436
  504.3 6.3 copy-start.27
  504.3 90.4 %copy-start.2 = (bf16[256,1024]{1,0:T(8,128)(2,1)S(1)}, bf16[256,1024]{1,0:T(8,128)(2,1)}, u32[]{:S(2)}) copy-start(bf16[256,1024]{1,0:T(8,128)(2,1)} %param.34) | copy-start | bytes 1572868
  504.3 90.4 %copy-start.4 = (bf16[1024,512]{1,0:T(8,128)(2,1)S(1)}, bf16[1024,512]{1,0:T(8,128)(2,1)}, u32[]{:S(2)}) copy-start(bf16[1024,512]{1,0:T(8,128)(2,1)} %param.30) | copy-start | bytes 3145732
  509.4 0.7 copy-start.6
  509.4 93.0 %copy-start.24 = (s32[256]{0:T(256)S(1)}, s32[256]{0:T(256)}, u32[]{:S(2)}) copy-start(s32[256]{0:T(256)} %param.35) | copy-start | bytes 3076
  510.7 7.1 %collective-permute-start = (bf16[64,8,64]{0,2,1:T(8,128)(2,1)S(1)}, bf16[64,8,64]{0,2,1:T(8,128)(2,1)S(1)}, u32[]{:S(2)}, u32[]{:S(2)}) collective-permute-start(bf16[64,8,64]{0,2,1:T(8,128)(2,1)S(1)} %multiply_convert_fusion.2), channel_id=1, source_target_pairs={{0,2},{2,4},{4,6},{6,8},{8,10},{10,12},{12,14},{14,16},{16,18},{18... | collective-permute-start | bytes 196616 | tf_op jit(solution)/shard_map/ppermute | solution.py:118
  517.8 7.1 %collective-permute-start.1 = (bf16[64,8,64]{0,2,1:T(8,128)(2,1)S(1)}, bf16[64,8,64]{0,2,1:T(8,128)(2,1)S(1)}, u32[]{:S(2)}, u32[]{:S(2)}) collective-permute-start(bf16[64,8,64]{0,2,1:T(8,128)(2,1)S(1)} %collective-permute-done), channel_id=1, source_target_pairs={{0,2},{2,4},{4,6},{6,8},{8,10},{10,12},{12,14},{14,16},{16,18},{18... | collective-permute-start | bytes 196616 | tf_op jit(solution)/shard_map/ppermute | solution.py:118
  519.5 110.8 %copy-start.28 = (f32[64]{0:T(128)S(1)}, f32[64]{0:T(128)}, u32[]{:S(2)}) copy-start(f32[64]{0:T(128)} %param.31) | copy-start | bytes 772
  519.6 142.4 %reduce-scatter.11.cloned.1.call-start = ((), (), s32[]{:S(2)}) async-start(), calls=%async_computation.9 | async-start | bytes 1572864 | tf_op jit(solution)/shard_map/reduce_scatter | solution.py:144
  524.9 7.2 %collective-permute-start.2 = (bf16[64,8,64]{0,2,1:T(8,128)(2,1)S(1)}, bf16[64,8,64]{0,2,1:T(8,128)(2,1)S(1)}, u32[]{:S(2)}, u32[]{:S(2)}) collective-permute-start(bf16[64,8,64]{0,2,1:T(8,128)(2,1)S(1)} %collective-permute-done.1), channel_id=1, source_target_pairs={{0,2},{2,4},{4,6},{6,8},{8,10},{10,12},{12,14},{14,16},{16,18},{18... | collective-permute-start | bytes 196616 | tf_op jit(solution)/shard_map/ppermute | solution.py:118
  532.1 85.2 %copy-start.7 = (bf16[64,8,64]{0,2,1:T(8,128)(2,1)}, bf16[64,8,64]{0,2,1:T(8,128)(2,1)S(1)}, u32[]{:S(2)}) copy-start(bf16[64,8,64]{0,2,1:T(8,128)(2,1)S(1)} %collective-permute-done.2) | copy-start | bytes 196612
  532.1 7.8 %collective-permute-start.3 = (bf16[64,8,64]{0,2,1:T(8,128)(2,1)S(1)}, bf16[64,8,64]{0,2,1:T(8,128)(2,1)S(1)}, u32[]{:S(2)}, u32[]{:S(2)}) collective-permute-start(bf16[64,8,64]{0,2,1:T(8,128)(2,1)S(1)} %collective-permute-done.2), channel_id=1, source_target_pairs={{0,2},{2,4},{4,6},{6,8},{8,10},{10,12},{12,14},{14,16},{16,18},{18... | collective-permute-start | bytes 196616 | tf_op jit(solution)/shard_map/ppermute | solution.py:118
  539.9 77.4 %copy-start.8 = (bf16[64,8,64]{0,2,1:T(8,128)(2,1)}, bf16[64,8,64]{0,2,1:T(8,128)(2,1)S(1)}, u32[]{:S(2)}) copy-start(bf16[64,8,64]{0,2,1:T(8,128)(2,1)S(1)} %collective-permute-done.3) | copy-start | bytes 196612
  539.9 7.1 %collective-permute-start.4 = (bf16[64,8,64]{0,2,1:T(8,128)(2,1)S(1)}, bf16[64,8,64]{0,2,1:T(8,128)(2,1)S(1)}, u32[]{:S(2)}, u32[]{:S(2)}) collective-permute-start(bf16[64,8,64]{0,2,1:T(8,128)(2,1)S(1)} %collective-permute-done.3), channel_id=1, source_target_pairs={{0,2},{2,4},{4,6},{6,8},{8,10},{10,12},{12,14},{14,16},{16,18},{18... | collective-permute-start | bytes 196616 | tf_op jit(solution)/shard_map/ppermute | solution.py:118
  547.0 0.7 copy-start.9
  547.7 8.3 %collective-permute-start.5 = (bf16[64,8,64]{0,2,1:T(8,128)(2,1)S(1)}, bf16[64,8,64]{0,2,1:T(8,128)(2,1)S(1)}, u32[]{:S(2)}, u32[]{:S(2)}) collective-permute-start(bf16[64,8,64]{0,2,1:T(8,128)(2,1)S(1)} %collective-permute-done.4), channel_id=1, source_target_pairs={{0,2},{2,4},{4,6},{6,8},{8,10},{10,12},{12,14},{14,16},{16,18},{18... | collective-permute-start | bytes 196616 | tf_op jit(solution)/shard_map/ppermute | solution.py:118
  556.0 0.7 copy-start.10
  556.6 7.1 %collective-permute-start.6 = (bf16[64,8,64]{0,2,1:T(8,128)(2,1)S(1)}, bf16[64,8,64]{0,2,1:T(8,128)(2,1)S(1)}, u32[]{:S(2)}, u32[]{:S(2)}) collective-permute-start(bf16[64,8,64]{0,2,1:T(8,128)(2,1)S(1)} %collective-permute-done.5), channel_id=1, source_target_pairs={{0,2},{2,4},{4,6},{6,8},{8,10},{10,12},{12,14},{14,16},{16,18},{18... | collective-permute-start | bytes 196616 | tf_op jit(solution)/shard_map/ppermute | solution.py:118
  564.4 7.1 %collective-permute-start.7 = (bf16[64,8,64]{0,2,1:T(8,128)(2,1)S(1)}, bf16[64,8,64]{0,2,1:T(8,128)(2,1)S(1)}, u32[]{:S(2)}, u32[]{:S(2)}) collective-permute-start(bf16[64,8,64]{0,2,1:T(8,128)(2,1)S(1)} %collective-permute-done.6), channel_id=1, source_target_pairs={{0,2},{2,4},{4,6},{6,8},{8,10},{10,12},{12,14},{14,16},{16,18},{18... | collective-permute-start | bytes 196616 | tf_op jit(solution)/shard_map/ppermute | solution.py:118
  571.5 0.7 copy-start.12
  572.1 7.1 %collective-permute-start.8 = (bf16[64,8,64]{0,2,1:T(8,128)(2,1)S(1)}, bf16[64,8,64]{0,2,1:T(8,128)(2,1)S(1)}, u32[]{:S(2)}, u32[]{:S(2)}) collective-permute-start(bf16[64,8,64]{0,2,1:T(8,128)(2,1)S(1)} %collective-permute-done.7), channel_id=1, source_target_pairs={{0,2},{2,4},{4,6},{6,8},{8,10},{10,12},{12,14},{14,16},{16,18},{18... | collective-permute-start | bytes 196616 | tf_op jit(solution)/shard_map/ppermute | solution.py:118
  579.2 0.7 copy-start.13
  579.9 7.1 %collective-permute-start.9 = (bf16[64,8,64]{0,2,1:T(8,128)(2,1)S(1)}, bf16[64,8,64]{0,2,1:T(8,128)(2,1)S(1)}, u32[]{:S(2)}, u32[]{:S(2)}) collective-permute-start(bf16[64,8,64]{0,2,1:T(8,128)(2,1)S(1)} %collective-permute-done.8), channel_id=1, source_target_pairs={{0,2},{2,4},{4,6},{6,8},{8,10},{10,12},{12,14},{14,16},{16,18},{18... | collective-permute-start | bytes 196616 | tf_op jit(solution)/shard_map/ppermute | solution.py:118
  587.6 7.1 %collective-permute-start.10 = (bf16[64,8,64]{0,2,1:T(8,128)(2,1)S(1)}, bf16[64,8,64]{0,2,1:T(8,128)(2,1)S(1)}, u32[]{:S(2)}, u32[]{:S(2)}) collective-permute-start(bf16[64,8,64]{0,2,1:T(8,128)(2,1)S(1)} %collective-permute-done.9), channel_id=1, source_target_pairs={{0,2},{2,4},{4,6},{6,8},{8,10},{10,12},{12,14},{14,16},{16,18},{18... | collective-permute-start | bytes 196616 | tf_op jit(solution)/shard_map/ppermute | solution.py:118
  594.7 1.4 copy-start.15
  594.7 7.1 %collective-permute-start.11 = (bf16[64,8,64]{0,2,1:T(8,128)(2,1)S(1)}, bf16[64,8,64]{0,2,1:T(8,128)(2,1)S(1)}, u32[]{:S(2)}, u32[]{:S(2)}) collective-permute-start(bf16[64,8,64]{0,2,1:T(8,128)(2,1)S(1)} %collective-permute-done.10), channel_id=1, source_target_pairs={{0,2},{2,4},{4,6},{6,8},{8,10},{10,12},{12,14},{14,16},{16,18},{18... | collective-permute-start | bytes 196616 | tf_op jit(solution)/shard_map/ppermute | solution.py:118
  601.8 0.7 copy-start.16
  602.4 7.1 %collective-permute-start.12 = (bf16[64,8,64]{0,2,1:T(8,128)(2,1)S(1)}, bf16[64,8,64]{0,2,1:T(8,128)(2,1)S(1)}, u32[]{:S(2)}, u32[]{:S(2)}) collective-permute-start(bf16[64,8,64]{0,2,1:T(8,128)(2,1)S(1)} %collective-permute-done.11), channel_id=1, source_target_pairs={{0,2},{2,4},{4,6},{6,8},{8,10},{10,12},{12,14},{14,16},{16,18},{18... | collective-permute-start | bytes 196616 | tf_op jit(solution)/shard_map/ppermute | solution.py:118
  610.2 7.1 %collective-permute-start.13 = (bf16[64,8,64]{0,2,1:T(8,128)(2,1)S(1)}, bf16[64,8,64]{0,2,1:T(8,128)(2,1)S(1)}, u32[]{:S(2)}, u32[]{:S(2)}) collective-permute-start(bf16[64,8,64]{0,2,1:T(8,128)(2,1)S(1)} %collective-permute-done.12), channel_id=1, source_target_pairs={{0,2},{2,4},{4,6},{6,8},{8,10},{10,12},{12,14},{14,16},{16,18},{18... | collective-permute-start | bytes 196616 | tf_op jit(solution)/shard_map/ppermute | solution.py:118
  617.3 0.6 copy-start.18
  617.3 7.2 %collective-permute-start.14 = (bf16[64,8,64]{0,2,1:T(8,128)(2,1)S(1)}, bf16[64,8,64]{0,2,1:T(8,128)(2,1)}, u32[]{:S(2)}, u32[]{:S(2)}) collective-permute-start(bf16[64,8,64]{0,2,1:T(8,128)(2,1)S(1)} %collective-permute-done.13), channel_id=1, source_target_pairs={{0,2},{2,4},{4,6},{6,8},{8,10},{10,12},{12,14},{14,16},{16,18},{18... | collective-permute-start | bytes 196616 | tf_op jit(solution)/shard_map/ppermute | solution.py:118
  630.4 6.7 %copy-start.21 = (pred[256,1024]{1,0:T(8,128)(4,1)S(1)}, pred[256,1024]{1,0:T(8,128)(4,1)}, u32[]{:S(2)}) copy-start(pred[256,1024]{1,0:T(8,128)(4,1)} %fusion.37) | copy-start | bytes 786436
  637.1 24.9 %copy-start.3 = (bf16[256,1024]{1,0:T(8,128)(2,1)S(1)}, bf16[256,1024]{1,0:T(8,128)(2,1)}, u32[]{:S(2)}) copy-start(bf16[256,1024]{1,0:T(8,128)(2,1)} %param.34) | copy-start | bytes 1572868
  (3 other events, 1.9 us)
Sparse Core Ops, SparseCore 0:
  10.7 53.1 all-gather.2
  207.5 84.7 all-reduce.2
  295.9 57.6 reduce-scatter.12
  357.6 102.7 reduce-scatter.6
  470.5 20.0 reduce-scatter.8
  519.7 43.4 all-gather.4
  644.3 17.5 reduce-scatter.10
